TPU v7x, 32 devices: a whole 2x2x4 slice. The times are simulated.
32 devices in a mesh: dp: 16 (over z, x, core), tensor: 2 (over y).
Axes of the slice: x: 2, y: 2, z: 4, core: 2. Of those that a mesh axis runs over, the one named last changes fastest.
Arguments:
- activations: bfloat16 [4096, 2880], P(('dp', 'tensor')), parts along dimension 0, may hold values from -6 to 6
- segment_ids: int32 [4096], P('dp'), parts along dimension 0, may hold values from 0 to 3, as said below
- attn_gain: float32 [2880], replicated, may hold values from 0.1 to 1.9
- qkv_weight: bfloat16 [2880, 5120], P(None, 'tensor'), may hold values from -2 to 2
- out_weight: bfloat16 [4096, 2880], P('tensor'), may hold values from -0.09375 to 0.09375
- ffn_gain: float32 [2880], replicated, may hold values from 0.1 to 1.9
- gate_weight: bfloat16 [2880, 2048], P(None, 'tensor'), may hold values from -0.109375 to 0.109375
- up_weight: bfloat16 [2880, 2048], P(None, 'tensor'), may hold values from -0.109375 to 0.109375
- down_weight: bfloat16 [2048, 2880], P('tensor'), may hold values from -0.125 to 0.125
Outputs:
- layer_out: bfloat16 [4096, 2880], P(('dp', 'tensor')), parts along dimension 0
There are 16 independent parts, one for each index of `dp`. A program takes and returns all parts, laid end to end along the dimension named above; an argument that names none is the same for every part. Nothing has to cross between parts.
Inputs may be any that keep to these rules, and one draw needn't show every extreme that they name: `segment_ids`: segment numbers never fall along the tokens, and each of the four segments holds at least one token.
All inputs are finite; a program needn't handle non-finite values.
Results may differ from a plain program's by a relative error of at most 0.035.
Values may be sent and summed in bfloat16 or wider, within the bound.
No kernel may reach another device: no remote copies, remote signals or barrier semaphores. Data moves between devices by JAX's collectives and lax.ppermute only.
A program may use at most 128 MiB of HBM per device.

v0:
```python
import jax
import jax.numpy as jnp
from jax import lax
from jax.sharding import PartitionSpec as P

HEADS = 64
KV_HEADS = 8
HEAD_DIM = 64


def normalize(rows_in, gain):
    floats = rows_in.astype(jnp.float32)
    mean_square = jnp.mean(floats * floats, axis=-1, keepdims=True)
    return (floats * lax.rsqrt(mean_square + 1e-05) * gain).astype(jnp.bfloat16)


def attend(projected, segment_ids):
    token_count = projected.shape[0]
    group_size = HEADS // KV_HEADS
    heads_view = projected.reshape(token_count, -1, group_size + 2, HEAD_DIM)
    key_rows = heads_view[:, :, group_size]
    value_rows = heads_view[:, :, group_size + 1]
    block_rows = token_count if token_count <= 512 else 512
    block_count = token_count // block_rows
    positions = jnp.arange(token_count, dtype=jnp.int32)

    def one_block(block_index):
        first_row = block_index * block_rows
        query_rows = lax.dynamic_slice_in_dim(heads_view, first_row, block_rows, 0)[
            :, :, :group_size
        ]
        query_pos = first_row + jnp.arange(block_rows, dtype=jnp.int32)
        query_seg = lax.dynamic_slice_in_dim(segment_ids, first_row, block_rows, 0)
        scores = jnp.einsum(
            "sngd,tnd->ngst", query_rows, key_rows, preferred_element_type=jnp.float32
        ) * HEAD_DIM ** (-0.5)
        allowed = (positions[None, :] <= query_pos[:, None]) & (
            segment_ids[None, :] == query_seg[:, None]
        )
        scores = jnp.where(allowed, scores, -1e30)
        row_max = jnp.max(scores, axis=-1, keepdims=True)
        weights = jnp.exp(scores - row_max)
        row_total = jnp.sum(weights, axis=-1, keepdims=True)
        softmax_out = (weights / row_total).astype(jnp.bfloat16)
        mixed = jnp.einsum(
            "ngst,tnd->sngd", softmax_out, value_rows, preferred_element_type=jnp.float32
        )
        return mixed.astype(jnp.bfloat16)

    blocks_out = lax.map(one_block, jnp.arange(block_count, dtype=jnp.int32))
    return blocks_out.reshape(token_count, -1)


def shards(
    activations,
    segment_ids,
    attn_gain,
    qkv_weight,
    out_weight,
    ffn_gain,
    gate_weight,
    up_weight,
    down_weight,
):
    own_rows = activations.shape[0]
    whole_rows = lax.all_gather(activations, "tensor", axis=0, tiled=True)
    projected = jnp.dot(
        normalize(whole_rows, attn_gain), qkv_weight, preferred_element_type=jnp.float32
    ).astype(jnp.bfloat16)
    mixed_heads = attend(projected, segment_ids)
    head_total = lax.psum(
        jnp.dot(mixed_heads, out_weight, preferred_element_type=jnp.float32).astype(jnp.bfloat16),
        "tensor",
    ).astype(jnp.float32)
    resid_whole = (whole_rows.astype(jnp.float32) + head_total).astype(jnp.bfloat16)
    shard_rows = normalize(resid_whole, ffn_gain)
    gate_act = jnp.dot(shard_rows, gate_weight, preferred_element_type=jnp.float32)
    up_act = jnp.dot(shard_rows, up_weight, preferred_element_type=jnp.float32)
    hidden = (jax.nn.silu(gate_act) * up_act).astype(jnp.bfloat16)
    resid_sum = lax.dynamic_slice_in_dim(
        resid_whole, lax.axis_index("tensor") * own_rows, own_rows, 0
    )
    ffn_out = lax.psum_scatter(
        jnp.dot(hidden, down_weight, preferred_element_type=jnp.float32).astype(jnp.bfloat16),
        "tensor",
        scatter_dimension=0,
        tiled=True,
    ).astype(jnp.float32)
    return (resid_sum.astype(jnp.float32) + ffn_out).astype(jnp.bfloat16)


def solution(mesh):
    placed = (
        P(("dp", "tensor"), None),
        P("dp"),
        P(),
        P(None, "tensor"),
        P("tensor", None),
        P(),
        P(None, "tensor"),
        P(None, "tensor"),
        P("tensor", None),
    )
    return jax.shard_map(
        shards, mesh=mesh, in_specs=placed, out_specs=P(("dp", "tensor"), None), check_vma=False
    )
```

profile of v0, /device:TPU:0, one launch (start us, length us, event | category | flops | bytes accessed | tf_op | source)
XLA Modules:
  0.0 167.5 jit_solution(3976080794666431789)
XLA Ops:
  6.5 0.0 all-gather.2.cloned.1.call-start
  6.5 0.7 all-gather.2.cloned.1.call-update
  7.3 0.0 all-reduce.2.cloned.1.call-start
  7.3 0.9 fusion.25
  8.2 29.5 %all-gather.2.cloned.1.call-done = bf16[256,2880]{0,1:T(8,128)(2,1)} async-done(((bf16[128,2880]{0,1:T(8,128)(2,1)}), bf16[256,2880]{0,1:T(8,128)(2,1)}) %all-gather.2.cloned.1.call-update) | async-done | bytes 1474576 | tf_op jit(solution)/shard_map/all_gather | solution.py:66
  37.7 1.8 %fusion.9 = f32[256]{0:T(256)S(1)} fusion(bf16[256,2880]{0,1:T(8,128)(2,1)} %all-gather.2.cloned.1.call-done), kind=kLoop, calls=%fused_computation.20 | loop fusion | flops 2211584 | bytes 1475584 | tf_op jit(solution)/shard_map/reduce_sum | solution.py:13
  39.5 10.0 %convolution_convert_fusion.2 = bf16[256,2560]{1,0:T(8,128)(2,1)S(1)} fusion(bf16[2880,2560]{1,0:T(8,128)(2,1)} %param.12, bf16[256,2880]{0,1:T(8,128)(2,1)} %all-gather.2.cloned.1.call-done, f32[2880]{0:T(1024)} %param.11, f32[256]{0:T(256)S(1)} %add_rsqrt_fusion.1), kind=kOutput, calls=%fused_computation.14 | convolution fusion | flops 3778478080 | bytes 17543424 | tf_op jit(solution)/shard_map/dot_general | solution.py:67
  49.5 0.6 copy.18
  50.1 1.3 fusion.18
  51.4 0.0 slice-start
  51.4 0.0 slice-start.1
  51.4 5.1 %fusion.30 = (f32[4,8,256]{2,1,0:T(8,128)S(1)}, f32[4,8,256,256]{2,3,1,0:T(8,128)}) fusion(f32[4,256,256,8]{2,1,3,0:T(8,128)S(1)} %fusion.18, pred[256,256]{0,1:T(8,128)(4,1)S(1)} %fusion.25), kind=kOutput, calls=%fused_computation.43 | output fusion | flops 12583167 | bytes 16875520 | tf_op jit(solution)/shard_map/while/body/eval_jaxpr/sub | solution.py:42
  56.5 0.0 slice-start.2
  56.5 4.4 %fusion.13 = bf16[4,64,8,256]{3,1,2,0:T(8,128)(2,1)S(1)} fusion(f32[4,8,256,256]{2,3,1,0:T(8,128)} %get-tuple-element.20, f32[4,8,256]{2,1,0:T(8,128)S(1)} %get-tuple-element.19, bf16[256,4,10,64]{0,3,2,1:T(8,128)(2,1)S(1)} %bitcast.39), kind=kOutput, calls=%fused_computation.24 | convolution fusion | flops 273154048 | bytes 9601024 | tf_op jit(solution)/shard_map/while/body/eval_jaxpr/ngst,tnd->sngd/dot_general | solution.py:45
  60.9 0.0 slice-done
  60.9 0.0 slice-done.1
  60.9 0.3 slice-done.2
  61.2 0.0 copy-start
  61.2 4.3 %convolution_convert_fusion = bf16[256,2880]{0,1:T(8,128)(2,1)} fusion(bf16[2048,2880]{0,1:T(8,128)(2,1)S(1)} %bitcast.41, bf16[256,2048]{0,1:T(8,128)(2,1)S(1)} %bitcast.42), kind=kOutput, calls=%fused_computation.12 | convolution fusion | flops 3020636160 | bytes 14319616 | tf_op jit(solution)/shard_map/dot_general | solution.py:72
  65.6 0.0 all-reduce.2.cloned.1.call-update
  65.6 0.2 reduce-scatter.4.cloned.1.call-start
  65.8 49.3 %all-reduce.2.cloned.1.call-done = bf16[256,2880]{0,1:T(8,128)(2,1)} async-done(((bf16[256,2880]{0,1:T(8,128)(2,1)}), bf16[256,2880]{0,1:T(8,128)(2,1)}) %all-reduce.2.cloned.1.call-update) | async-done | bytes 1474576 | tf_op jit(solution)/shard_map/psum | solution.py:71
  115.1 0.0 copy-done
  115.1 2.0 %fusion.6 = (f32[256]{0:T(256)S(1)}, bf16[256,2880]{0,1:T(8,128)(2,1)S(1)}) fusion(bf16[256,2880]{0,1:T(8,128)(2,1)} %all-reduce.2.cloned.1.call-done, bf16[256,2880]{0,1:T(8,128)(2,1)S(1)} %copy-done), kind=kLoop, calls=%fused_computation.17 | loop fusion | flops 5160704 | bytes 4424704 | tf_op jit(solution)/shard_map/reduce_sum | solution.py:13
  117.2 0.0 copy-done.1
  117.2 5.6 %fusion.23 = f32[256,1024]{1,0:T(8,128)} fusion(bf16[2880,1024]{1,0:T(8,128)(2,1)} %param.15, bf16[256,2880]{0,1:T(8,128)(2,1)S(1)} %get-tuple-element.18, f32[2880]{0:T(1024)S(1)} %copy-done.1, f32[256]{0:T(256)S(1)} %add_rsqrt_fusion), kind=kOutput, calls=%fused_computation.33 | convolution fusion | flops 1512898560 | bytes 8433920 | tf_op jit(solution)/shard_map/dot_general | solution.py:77
  122.7 8.3 %convolution_convert_fusion.1 = bf16[256,2880]{0,1:T(8,128)(2,1)S(1)} fusion(bf16[1024,2880]{0,1:T(8,128)(2,1)} %param.17, bf16[2880,1024]{1,0:T(8,128)(2,1)} %param.16, f32[256,1024]{1,0:T(8,128)} %fusion.23, bf16[256,2880]{0,1:T(8,128)(2,1)S(1)} %get-tuple-element.18, f32[2880]{0:T(1024)S(1)} %copy-done.1, f32[256]{0:T(256)S(1)} %add_rsqrt_fusion), kind=kOutput, calls=%fused_computation.13 | convolution fusion | flops 3025158144 | bytes 15806720 | tf_op jit(solution)/shard_map/dot_general | solution.py:84
  131.1 1.7 %copy.25 = bf16[256,2880]{1,0:T(8,128)(2,1)} copy(bf16[256,2880]{0,1:T(8,128)(2,1)S(1)} %convolution_convert_fusion.1) | data formatting | bytes 2949120
  132.8 0.0 reduce-scatter.4.cloned.1.call-update
  132.8 25.6 %reduce-scatter.4.cloned.1.call-done = bf16[128,2880]{1,0:T(8,128)(2,1)} async-done(((bf16[256,2880]{1,0:T(8,128)(2,1)}), bf16[128,2880]{1,0:T(8,128)(2,1)}) %reduce-scatter.4.cloned.1.call-update) | async-done | bytes 737296
  158.4 1.5 copy.26
  159.9 1.1 add_convert_fusion
  (4 shorter events, 0.0 us)
Async XLA Ops:
  6.5 31.1 %all-gather.2.cloned.1.call-start = ((), (), s32[]{:S(2)}) async-start(), calls=%async_computation.1 | async-start | bytes 2211840 | tf_op jit(solution)/shard_map/all_gather | solution.py:66
  7.3 107.9 %all-reduce.2.cloned.1.call-start = ((), (), s32[]{:S(2)}) async-start(), calls=%async_computation.2 | async-start | bytes 2949120 | tf_op jit(solution)/shard_map/psum | solution.py:71
  51.4 9.5 %slice-start = ((s8[11796480]{0:T(1024)(128)(4,1)}), s8[3407872]{0:T(1024)(128)(4,1)S(1)}, s32[]{:S(2)}) async-start(s8[11796480]{0:T(1024)(128)(4,1)} %bitcast.40), calls=%async_computation.4 | async-start | bytes 6815744
  51.4 9.5 %slice-start.1 = ((s8[11796480]{0:T(1024)(128)(4,1)}), s8[4194304]{0:T(1024)(128)(4,1)S(1)}, s32[]{:S(2)}) async-start(s8[11796480]{0:T(1024)(128)(4,1)} %bitcast.40), calls=%async_computation.5 | async-start | bytes 8388608
  56.5 4.7 %slice-start.2 = ((s8[11796480]{0:T(1024)(128)(4,1)}), s8[4194304]{0:T(1024)(128)(4,1)S(1)}, s32[]{:S(2)}) async-start(s8[11796480]{0:T(1024)(128)(4,1)} %bitcast.40), calls=%async_computation.6 | async-start | bytes 8388608
  61.2 53.9 %copy-start = (bf16[256,2880]{0,1:T(8,128)(2,1)S(1)}, bf16[256,2880]{0,1:T(8,128)(2,1)}, u32[]{:S(2)}) copy-start(bf16[256,2880]{0,1:T(8,128)(2,1)} %all-gather.2.cloned.1.call-done) | copy-start | bytes 4423684
  65.6 51.6 %copy-start.1 = (f32[2880]{0:T(1024)S(1)}, f32[2880]{0:T(1024)}, u32[]{:S(2)}) copy-start(f32[2880]{0:T(1024)} %param.14) | copy-start | bytes 34564
  65.6 92.8 %reduce-scatter.4.cloned.1.call-start = ((), (), s32[]{:S(2)}) async-start(), calls=%async_computation.3 | async-start | bytes 2260992
Sparse Core Ops, SparseCore 0:
  8.9 28.7 all-gather.1
  65.7 49.3 all-reduce.1
  132.9 25.4 reduce-scatter.3
where the time goes:
time: 168 us; the launch traced here: 167 us
  waiting for transfers between devices  105 us (62%)
  matrix products  33.9 us (20%)
  between operations  13.2 us (8%)
  other arithmetic  10.8 us (6%)
  local copies, waits for them, and re-layouts  4.19 us (2%)
    psum x1, waiting for transfers between devices, shards(): lax.psum(jnp.dot(mixed_heads, out_weight, preferred_element_type=jnp.floa...  49.3 us
    all_gather x1, waiting for transfers between devices, shards(): whole_rows = lax.all_gather(activations, 'tensor', axis=0, tiled=True)  29.5 us
    unnamed x4, waiting for transfers between devices  26.3 us
    dot_general x1, matrix products, shards(): jnp.dot(normalize(whole_rows, attn_gain), qkv_weight, preferred_element_t...  10 us
    dot_general x1, matrix products, shards(): jnp.dot(hidden, down_weight, preferred_element_type=jnp.float32)  8.33 us
    dot_general x1, matrix products, shards(): jnp.dot(shard_rows, gate_weight, preferred_element_type=jnp.float32)  5.56 us
    sub x1, other arithmetic, one_block(): weights = jnp.exp(scores - row_max)  5.08 us
    dot_general x1, matrix products, one_block(): jnp.einsum('ngst,tnd->sngd', softmax_out, value_rows, preferred_element_t...  4.38 us
  transfers between devices with their start and end apart: 3, of which 3 were waited for; matrix products, arithmetic and copies ran while one was open for 1% of the time, Pallas kernels for 0%

commit v1 on v0

--- a/solution.py
+++ b/solution.py
@@ -68,10 +68,16 @@
         normalize(whole_rows, attn_gain), qkv_weight, preferred_element_type=jnp.float32
     ).astype(jnp.bfloat16)
     mixed_heads = attend(projected, segment_ids)
-    head_total = lax.psum(
-        jnp.dot(mixed_heads, out_weight, preferred_element_type=jnp.float32).astype(jnp.bfloat16),
-        "tensor",
-    ).astype(jnp.float32)
+    head_total = (
+        lax.all_gather(
+            jnp.dot(mixed_heads, out_weight, preferred_element_type=jnp.float32).astype(
+                jnp.bfloat16
+            ),
+            axis_name="tensor",
+        )
+        .sum(axis=0)
+        .astype(jnp.float32)
+    )
     resid_whole = (whole_rows.astype(jnp.float32) + head_total).astype(jnp.bfloat16)
     shard_rows = normalize(resid_whole, ffn_gain)
     gate_act = jnp.dot(shard_rows, gate_weight, preferred_element_type=jnp.float32)

time: 168 us -> 182 us (1.083)
  other arithmetic: 10.8 us -> 24.5 us
  local copies, waits for them, and re-layouts: 4.19 us -> 12.3 us
  waiting for transfers between devices: 105 us -> 98.4 us
    psum x1 -> x0, waiting for transfers between devices: 49.3 us -> none  [shards(): lax.psum(jnp.dot(mixed_heads, out_weight, preferred_element_type=jnp.floa...]
    all_gather x0 -> x1, waiting for transfers between devices: none -> 42.6 us  [shards(): lax.all_gather(jnp.dot(mixed_heads, out_weight, preferred_element_type=jn...]
    reduce_sum x0 -> x1, other arithmetic: none -> 15.1 us  [shards(): head_total = lax.all_gather(jnp.dot(mixed_heads, out_weight, preferred_el...]
    all_gather x0 -> x1, local copies, waits for them, and re-layouts: none -> 7.04 us  [shards(): lax.all_gather(jnp.dot(mixed_heads, out_weight, preferred_element_type=jn...]
    unnamed x12 -> x16, local copies, waits for them, and re-layouts: 3.57 us -> 4.69 us
  transfers between devices with their start and end apart: 3 -> 3, of which waited for: 3 -> 3; matrix products, arithmetic and copies ran while one was open for 1% -> 0% of each run, Pallas kernels for 0% -> 0%
where the time goes in v1:
time: 182 us
  waiting for transfers between devices  98.4 us (54%)
  matrix products  33.1 us (18%)
  other arithmetic  24.5 us (13%)
  between operations  13.2 us (7%)
  local copies, waits for them, and re-layouts  12.3 us (7%)
    all_gather x1, waiting for transfers between devices, shards(): lax.all_gather(jnp.dot(mixed_heads, out_weight, preferred_element_type=jn...  42.6 us
    all_gather x1, waiting for transfers between devices, shards(): whole_rows = lax.all_gather(activations, 'tensor', axis=0, tiled=True)  29.5 us
    unnamed x4, waiting for transfers between devices  26.3 us
    reduce_sum x1, other arithmetic, shards(): head_total = lax.all_gather(jnp.dot(mixed_heads, out_weight, preferred_el...  15.1 us
    dot_general x1, matrix products, shards(): jnp.dot(normalize(whole_rows, attn_gain), qkv_weight, preferred_element_t...  10 us
    dot_general x1, matrix products, shards(): jnp.dot(hidden, down_weight, preferred_element_type=jnp.float32)  8.5 us
    all_gather x1, local copies, waits for them, and re-layouts, shards(): lax.all_gather(jnp.dot(mixed_heads, out_weight, preferred_element_type=jn...  7.04 us
    sub x1, other arithmetic, one_block(): weights = jnp.exp(scores - row_max)  5.08 us
  transfers between devices with their start and end apart: 3, of which 3 were waited for; matrix products, arithmetic and copies ran while one was open for 0% of the time, Pallas kernels for 0%

profile of v1, /device:TPU:0, one launch (start us, length us, event | category | flops | bytes accessed | tf_op | source)
XLA Modules:
  0.0 181.9 jit_solution(12478699107135717071)
XLA Ops:
  6.5 0.0 all-gather.4.cloned.1.call-start
  6.5 0.7 all-gather.4.cloned.1.call-update
  7.3 0.0 all-gather.6.cloned.1.call-start
  7.3 0.9 fusion.25
  8.2 29.5 %all-gather.4.cloned.1.call-done = bf16[256,2880]{0,1:T(8,128)(2,1)} async-done(((bf16[128,2880]{0,1:T(8,128)(2,1)}), bf16[256,2880]{0,1:T(8,128)(2,1)}) %all-gather.4.cloned.1.call-update) | async-done | bytes 1474576 | tf_op jit(solution)/shard_map/all_gather | solution.py:66
  37.7 1.8 fusion.9
  39.5 10.0 %convolution_convert_fusion.2 = bf16[256,2560]{1,0:T(8,128)(2,1)S(1)} fusion(bf16[2880,2560]{1,0:T(8,128)(2,1)} %param.12, bf16[256,2880]{0,1:T(8,128)(2,1)} %all-gather.4.cloned.1.call-done, f32[2880]{0:T(1024)} %param.11, f32[256]{0:T(256)S(1)} %add_rsqrt_fusion.1), kind=kOutput, calls=%fused_computation.14 | convolution fusion | flops 3778478080 | bytes 17543424 | tf_op jit(solution)/shard_map/dot_general | solution.py:67
  49.5 0.6 copy.18
  50.1 1.3 fusion.18
  51.4 0.0 slice-start
  51.4 0.0 slice-start.1
  51.4 5.1 %fusion.30 = (f32[4,8,256]{2,1,0:T(8,128)S(1)}, f32[4,8,256,256]{2,3,1,0:T(8,128)}) fusion(f32[4,256,256,8]{2,1,3,0:T(8,128)S(1)} %fusion.18, pred[256,256]{0,1:T(8,128)(4,1)S(1)} %fusion.25), kind=kOutput, calls=%fused_computation.43 | output fusion | flops 12583167 | bytes 16875520 | tf_op jit(solution)/shard_map/while/body/eval_jaxpr/sub | solution.py:42
  56.5 4.4 %fusion.13 = bf16[4,64,8,256]{3,1,2,0:T(8,128)(2,1)S(1)} fusion(f32[4,8,256,256]{2,3,1,0:T(8,128)} %get-tuple-element.20, f32[4,8,256]{2,1,0:T(8,128)S(1)} %get-tuple-element.19, bf16[256,4,10,64]{0,3,2,1:T(8,128)(2,1)S(1)} %bitcast.41), kind=kOutput, calls=%fused_computation.24 | convolution fusion | flops 273154048 | bytes 9601024 | tf_op jit(solution)/shard_map/while/body/eval_jaxpr/ngst,tnd->sngd/dot_general | solution.py:45
  60.9 0.0 slice-done
  60.9 0.3 slice-done.2
  61.2 4.4 %convolution_convert_fusion = bf16[256,2880]{0,1:T(8,128)(2,1)} fusion(bf16[2048,2880]{0,1:T(8,128)(2,1)S(1)} %bitcast.43, bf16[256,2048]{0,1:T(8,128)(2,1)S(1)} %bitcast.44), kind=kOutput, calls=%fused_computation.12 | convolution fusion | flops 3020636160 | bytes 14319616 | tf_op jit(solution)/shard_map/dot_general | solution.py:73
  65.6 0.0 all-gather.6.cloned.1.call-update
  65.6 0.2 reduce-scatter.4.cloned.1.call-start
  65.8 42.6 %all-gather.6.cloned.1.call-done = bf16[512,2880]{0,1:T(8,128)(2,1)} async-done(((bf16[256,2880]{0,1:T(8,128)(2,1)}), bf16[512,2880]{0,1:T(8,128)(2,1)}) %all-gather.6.cloned.1.call-update) | async-done | bytes 2949136 | tf_op jit(solution)/shard_map/all_gather | solution.py:72
  108.4 7.0 %reshape.32 = bf16[2,256,2880]{1,0,2:T(2,128)(2,1)} reshape(bf16[512,2880]{0,1:T(8,128)(2,1)} %all-gather.6.cloned.1.call-done) | data formatting | bytes 5898240 | tf_op jit(solution)/shard_map/all_gather | solution.py:72
  115.5 15.1 %reduce_sum.42 = bf16[256,2880]{0,1:T(8,128)(2,1)S(1)} reduce(bf16[2,256,2880]{1,0,2:T(2,128)(2,1)} %reshape.32, bf16[]{:T(256)} %constant.42.clone.1), dimensions={0}, to_apply=%region_3.4 | reduce | flops 737280 | bytes 4423682 | tf_op jit(solution)/shard_map/reduce_sum | solution.py:78
  130.6 0.0 copy-done
  130.6 0.0 copy-start.3
  130.6 0.6 fusion.6
  131.3 1.1 copy-done.1
  132.4 4.6 %fusion.23 = f32[256,1024]{1,0:T(8,128)S(1)} fusion(bf16[2880,1024]{1,0:T(8,128)(2,1)} %param.15, bf16[256,2880]{0,1:T(8,128)(2,1)S(1)} %get-tuple-element.18, f32[2880]{0:T(1024)S(1)} %copy-done.3, f32[256]{0:T(256)S(1)} %add_rsqrt_fusion), kind=kOutput, calls=%fused_computation.33 | convolution fusion | flops 1512898560 | bytes 8433920 | tf_op jit(solution)/shard_map/dot_general | solution.py:83
  137.0 8.5 %convolution_convert_fusion.1 = bf16[256,2880]{0,1:T(8,128)(2,1)S(1)} fusion(bf16[1024,2880]{0,1:T(8,128)(2,1)} %param.17, bf16[2880,1024]{1,0:T(8,128)(2,1)} %param.16, f32[256,1024]{1,0:T(8,128)S(1)} %fusion.23, bf16[256,2880]{0,1:T(8,128)(2,1)} %copy-done.1, f32[2880]{0:T(1024)S(1)} %copy-done.3, f32[256]{0:T(256)S(1)} %add_rsqrt_fusion), kind=kOutput, calls=%fused_computation.13 | convolution fusion | flops 3025158144 | bytes 15806720 | tf_op jit(solution)/shard_map/dot_general | solution.py:90
  145.5 1.7 copy.25
  147.2 0.0 reduce-scatter.4.cloned.1.call-update
  147.2 25.6 %reduce-scatter.4.cloned.1.call-done = bf16[128,2880]{1,0:T(8,128)(2,1)} async-done(((bf16[256,2880]{1,0:T(8,128)(2,1)}), bf16[128,2880]{1,0:T(8,128)(2,1)}) %reduce-scatter.4.cloned.1.call-update) | async-done | bytes 737296
  172.8 1.5 copy.26
  174.3 1.1 add_convert_fusion
  (10 shorter events, 0.0 us)
Async XLA Ops:
  6.5 31.1 %all-gather.4.cloned.1.call-start = ((), (), s32[]{:S(2)}) async-start(), calls=%async_computation.1 | async-start | bytes 2211840 | tf_op jit(solution)/shard_map/all_gather | solution.py:66
  7.3 101.2 %all-gather.6.cloned.1.call-start = ((), (), s32[]{:S(2)}) async-start(), calls=%async_computation.2 | async-start | bytes 4423680 | tf_op jit(solution)/shard_map/all_gather | solution.py:72
  51.4 9.5 %slice-start = ((s8[11796480]{0:T(1024)(128)(4,1)}), s8[3407872]{0:T(1024)(128)(4,1)S(1)}, s32[]{:S(2)}) async-start(s8[11796480]{0:T(1024)(128)(4,1)} %bitcast.42), calls=%async_computation.4 | async-start | bytes 6815744
  51.4 9.5 %slice-start.1 = ((s8[11796480]{0:T(1024)(128)(4,1)}), s8[4194304]{0:T(1024)(128)(4,1)S(1)}, s32[]{:S(2)}) async-start(s8[11796480]{0:T(1024)(128)(4,1)} %bitcast.42), calls=%async_computation.5 | async-start | bytes 8388608
  56.5 4.7 %slice-start.2 = ((s8[11796480]{0:T(1024)(128)(4,1)}), s8[4194304]{0:T(1024)(128)(4,1)S(1)}, s32[]{:S(2)}) async-start(s8[11796480]{0:T(1024)(128)(4,1)} %bitcast.42), calls=%async_computation.6 | async-start | bytes 8388608
  65.6 107.2 %reduce-scatter.4.cloned.1.call-start = ((), (), s32[]{:S(2)}) async-start(), calls=%async_computation.3 | async-start | bytes 2260992
  115.5 15.1 %copy-start = (bf16[256,2880]{0,1:T(8,128)(2,1)S(1)}, bf16[256,2880]{0,1:T(8,128)(2,1)}, u32[]{:S(2)}) copy-start(bf16[256,2880]{0,1:T(8,128)(2,1)} %all-gather.4.cloned.1.call-done) | copy-start | bytes 4423684
  130.6 1.8 copy-start.3
  131.2 1.1 copy-start.1
  145.5 28.8 %copy-start.2 = (bf16[256,2880]{0,1:T(8,128)(2,1)S(1)}, bf16[256,2880]{0,1:T(8,128)(2,1)}, u32[]{:S(2)}) copy-start(bf16[256,2880]{0,1:T(8,128)(2,1)} %copy-done.1) | copy-start | bytes 4423684
Sparse Core Ops, SparseCore 0:
  8.9 28.7 all-gather.3
  65.7 42.6 all-gather.5
  147.4 25.4 reduce-scatter.3
